TPU v7x, 32 devices: a whole 2x2x4 slice. The times are simulated.
32 devices in a mesh: gx: 4 (over z), gy: 4 (over y, core), gz: 2 (over x).
Axes of the slice: x: 2, y: 2, z: 4, core: 2. Of those that a mesh axis runs over, the one named last changes fastest.
Arguments:
- volume: bfloat16 [32, 64, 32, 128], P('gx', 'gy', 'gz'), may hold values from -6 to 6
- w_full: bfloat16 [3, 3, 3, 128, 128], replicated, may hold values from -0.15625 to 0.15625
- w_half: bfloat16 [3, 3, 3, 128, 256], replicated, may hold values from -0.15625 to 0.15625
- w_bottom_in: bfloat16 [3, 3, 3, 256, 512], P(None, None, None, None, 'gx'), may hold values from -0.109375 to 0.109375
- w_bottom_out: bfloat16 [3, 3, 3, 512, 512], P(None, None, None, None, 'gx'), may hold values from -0.078125 to 0.078125
- w_up: bfloat16 [3, 3, 3, 768, 256], replicated, may hold values from -0.0625 to 0.0625
Outputs:
- decoded: bfloat16 [16, 32, 16, 256], P('gx', 'gy', 'gz')
All inputs are finite; a program needn't handle non-finite values.
Results may differ from a plain program's by a relative error of at most 0.009.
Values may be sent and summed in bfloat16 or wider, within the bound.
A program may use at most 64 MiB of HBM per device.

v0:
```python
import jax
import jax.numpy as jnp
from jax import lax
from jax.sharding import PartitionSpec as P


def with_halo(cells, sides, width):
    for axis, dim in sides:
        count = lax.axis_size(axis)
        ends = count - 1
        head = lax.slice_in_dim(cells, 0, width, axis=dim)
        tail = lax.slice_in_dim(cells, cells.shape[dim] - width, cells.shape[dim], axis=dim)
        cells = jnp.concatenate(
            [
                lax.ppermute(tail, axis, [(i, (i + 1) % count) for i in range(ends)]),
                cells,
                lax.ppermute(head, axis, [((i + 1) % count, i) for i in range(ends)]),
            ],
            axis=dim,
        )
    return cells


def convolve(padded, kernel):
    size_x = padded.shape[0] - 2
    size_y = padded.shape[1] - 2
    size_z = padded.shape[2] - 2
    channels = padded.shape[3]
    total = jnp.zeros((size_x * size_y * size_z, kernel.shape[4]), jnp.float32)
    for offset_x in range(3):
        for offset_y in range(3):
            for offset_z in range(3):
                window = padded[
                    offset_x : offset_x + size_x,
                    offset_y : offset_y + size_y,
                    offset_z : offset_z + size_z,
                    :,
                ]
                total = total + jnp.dot(
                    window.reshape(-1, channels),
                    kernel[offset_x, offset_y, offset_z],
                    preferred_element_type=jnp.float32,
                )
    return total.reshape(size_x, size_y, size_z, kernel.shape[4])


def rectify(total):
    return jnp.maximum(total, 0.0).astype(jnp.bfloat16)


def shrink(field):
    size_x, size_y, size_z, channels = field.shape
    blocks = field.reshape(size_x // 2, 2, size_y // 2, 2, size_z // 2, 2, channels)
    return jnp.max(blocks, axis=(1, 3, 5))


def enlarge(field):
    size_x, size_y, size_z, channels = field.shape
    spread = jnp.broadcast_to(
        field[:, None, :, None, :, None, :], (size_x, 2, size_y, 2, size_z, 2, channels)
    )
    return spread.reshape(2 * size_x, 2 * size_y, 2 * size_z, channels)


def pad_first(field):
    return jnp.pad(field, ((1, 1), (0, 0), (0, 0), (0, 0)))


def on_device(volume, w_full, w_half, w_bottom_in, w_bottom_out, w_up):
    padded = with_halo(volume, (("gx", 0), ("gy", 1), ("gz", 2)), 1)
    full_level = rectify(convolve(padded, w_full))
    pooled = shrink(full_level)
    pooled_rim = with_halo(pooled, (("gx", 0), ("gy", 1), ("gz", 2)), 1)
    skip_level = rectify(convolve(pooled_rim, w_half))
    coarse = shrink(skip_level)
    column = lax.all_gather(coarse, "gx", axis=0, tiled=True)
    column = with_halo(column, (("gy", 1), ("gz", 2)), 1)
    bottom_first = rectify(convolve(pad_first(column), w_bottom_in))
    filters = lax.all_gather(bottom_first, "gx", axis=3, tiled=True)
    filters = with_halo(filters, (("gy", 1), ("gz", 2)), 1)
    bottom_second = rectify(convolve(pad_first(filters), w_bottom_out))
    regrouped = lax.all_to_all(bottom_second, "gx", split_axis=0, concat_axis=3, tiled=True)
    joined = jnp.concatenate([enlarge(regrouped), skip_level], axis=3)
    joined = with_halo(joined, (("gx", 0), ("gy", 1), ("gz", 2)), 1)
    return convolve(joined, w_up).astype(jnp.bfloat16)


def solution(mesh):
    return jax.shard_map(
        on_device,
        mesh=mesh,
        in_specs=(
            P("gx", "gy", "gz", None),
            P(),
            P(),
            P(None, None, None, None, "gx"),
            P(None, None, None, None, "gx"),
            P(),
        ),
        out_specs=P("gx", "gy", "gz", None),
        check_vma=False,
    )
```

profile of v0, /device:TPU:3, one launch (start us, length us, event | category | flops | bytes accessed | tf_op | source)
XLA Modules:
  0.0 225.7 jit_solution(15556953054492281344)
XLA Ops:
  0.9 3.2 %collective-permute-start = (bf16[1,16,16,128]{3,2,1,0:T(8,128)(2,1)S(1)}, bf16[1,16,16,128]{3,2,1,0:T(8,128)(2,1)S(1)}, u32[]{:S(2)}, u32[]{:S(2)}) collective-permute-start(bf16[1,16,16,128]{3,2,1,0:T(8,128)(2,1)S(1)} %get-tuple-element.74), channel_id=1, source_target_pairs={{0,8},{8,16},{16,24},{1,9},{9,17},{17,25},{2,10},{10,18},{18,26},{... | collective-permute-start | bytes 196616 | tf_op jit(solution)/shard_map/ppermute | solution.py:15
  4.1 1.3 collective-permute-start.1
  5.4 3.7 %collective-permute-done.1 = bf16[1,16,16,128]{3,2,1,0:T(8,128)(2,1)S(1)} collective-permute-done((bf16[1,16,16,128]{3,2,1,0:T(8,128)(2,1)S(1)}, bf16[1,16,16,128]{3,2,1,0:T(8,128)(2,1)S(1)}, u32[]{:S(2)}, u32[]{:S(2)}) %collective-permute-start.1) | collective-permute-done | bytes 65568 | tf_op jit(solution)/shard_map/ppermute | solution.py:17
  9.1 1.8 pad_maximum_fusion.4
  11.0 5.1 %collective-permute-start.2 = (bf16[10,1,16,128]{3,2,1,0:T(8,128)(2,1)S(1)}, bf16[10,1,16,128]{3,2,1,0:T(8,128)(2,1)S(1)}, u32[]{:S(2)}, u32[]{:S(2)}) collective-permute-start(bf16[10,1,16,128]{3,2,1,0:T(8,128)(2,1)S(1)} %get-tuple-element.64), channel_id=1, source_target_pairs={{0,2},{2,4},{4,6},{1,3},{3,5},{5,7},{8,10},{10,12},{12,14},{9,11},... | collective-permute-start | bytes 122888 | tf_op jit(solution)/shard_map/ppermute | solution.py:15
  16.1 1.9 collective-permute-start.3
  18.0 3.4 %collective-permute-done.3 = bf16[10,1,16,128]{3,2,1,0:T(8,128)(2,1)S(1)} collective-permute-done((bf16[10,1,16,128]{3,2,1,0:T(8,128)(2,1)S(1)}, bf16[10,1,16,128]{3,2,1,0:T(8,128)(2,1)S(1)}, u32[]{:S(2)}, u32[]{:S(2)}) %collective-permute-start.3) | collective-permute-done | bytes 40992 | tf_op jit(solution)/shard_map/ppermute | solution.py:17
  21.6 1.3 collective-permute-start.4
  22.9 4.1 %collective-permute-start.5 = (bf16[10,18,1,128]{3,2,1,0:T(2,128)(2,1)S(1)}, bf16[10,18,1,128]{3,2,1,0:T(2,128)(2,1)S(1)}, u32[]{:S(2)}, u32[]{:S(2)}) collective-permute-start(bf16[10,18,1,128]{3,2,1,0:T(2,128)(2,1)S(1)} %get-tuple-element.48), channel_id=1, source_target_pairs={{1,0},{3,2},{5,4},{7,6},{9,8},{11,10},{13,12},{15,14},{17,16},{19,... | collective-permute-start | bytes 138248 | tf_op jit(solution)/shard_map/ppermute | solution.py:17
  29.5 2.6 %fusion.380 = (bf16[8,16,16,128]{3,2,1,0:T(8,128)(2,1)S(1)}, bf16[8,16,16,128]{3,2,1,0:T(8,128)(2,1)S(1)}, bf16[8,16,16,128]{3,2,1,0:T(8,128)(2,1)S(1)}, bf16[8,...) fusion(bf16[10,18,17,128]{3,2,1,0:T(8,128)(2,1)S(1)} %get-tuple, ...), kind=kLoop, calls=%fused_computation.565 | loop fusion | bytes 18874368 | tf_op jit(solution)/shard_map/slice | solution.py:33
  41.0 3.2 %collective-permute-start.6 = (bf16[1,8,8,128]{3,2,1,0:T(8,128)(2,1)S(1)}, bf16[1,8,8,128]{3,2,1,0:T(8,128)(2,1)S(1)}, u32[]{:S(2)}, u32[]{:S(2)}) collective-permute-start(bf16[1,8,8,128]{3,2,1,0:T(8,128)(2,1)S(1)} %get-tuple-element.181), channel_id=1, source_target_pairs={{0,8},{8,16},{16,24},{1,9},{9,17},{17,25},{2,10},{10,18},{18,26},{... | collective-permute-start | bytes 49160 | tf_op jit(solution)/shard_map/ppermute | solution.py:15
  44.2 1.3 collective-permute-start.7
  45.5 3.2 %collective-permute-done.7 = bf16[1,8,8,128]{3,2,1,0:T(8,128)(2,1)S(1)} collective-permute-done((bf16[1,8,8,128]{3,2,1,0:T(8,128)(2,1)S(1)}, bf16[1,8,8,128]{3,2,1,0:T(8,128)(2,1)S(1)}, u32[]{:S(2)}, u32[]{:S(2)}) %collective-permute-start.7) | collective-permute-done | bytes 16416 | tf_op jit(solution)/shard_map/ppermute | solution.py:17
  48.7 4.5 %collective-permute-start.8 = (bf16[6,1,8,128]{3,2,1,0:T(8,128)(2,1)S(1)}, bf16[6,1,8,128]{3,2,1,0:T(8,128)(2,1)S(1)}, u32[]{:S(2)}, u32[]{:S(2)}) collective-permute-start(bf16[6,1,8,128]{3,2,1,0:T(8,128)(2,1)S(1)} %get-tuple-element.172), channel_id=1, source_target_pairs={{0,2},{2,4},{4,6},{1,3},{3,5},{5,7},{8,10},{10,12},{12,14},{9,11},... | collective-permute-start | bytes 36872 | tf_op jit(solution)/shard_map/ppermute | solution.py:15
  53.2 1.9 collective-permute-start.9
  55.1 3.1 %collective-permute-done.9 = bf16[6,1,8,128]{3,2,1,0:T(8,128)(2,1)S(1)} collective-permute-done((bf16[6,1,8,128]{3,2,1,0:T(8,128)(2,1)S(1)}, bf16[6,1,8,128]{3,2,1,0:T(8,128)(2,1)S(1)}, u32[]{:S(2)}, u32[]{:S(2)}) %collective-permute-start.9) | collective-permute-done | bytes 12320 | tf_op jit(solution)/shard_map/ppermute | solution.py:17
  58.3 1.3 collective-permute-start.10
  59.6 4.0 %collective-permute-start.11 = (bf16[6,10,1,128]{3,2,1,0:T(2,128)(2,1)S(1)}, bf16[6,10,1,128]{3,2,1,0:T(2,128)(2,1)S(1)}, u32[]{:S(2)}, u32[]{:S(2)}) collective-permute-start(bf16[6,10,1,128]{3,2,1,0:T(2,128)(2,1)S(1)} %get-tuple-element.158), channel_id=1, source_target_pairs={{1,0},{3,2},{5,4},{7,6},{9,8},{11,10},{13,12},{15,14},{17,16},{19,... | collective-permute-start | bytes 46088 | tf_op jit(solution)/shard_map/ppermute | solution.py:17
  69.8 10.3 %all_gather.6 = bf16[8,4,4,256]{3,2,1,0:T(4,128)(2,1)S(1)} all-gather(bf16[2,4,4,256]{3,2,1,0:T(4,128)(2,1)S(1)} %reduce_max.19), channel_id=1, replica_groups=mesh['gx'=4,'gy'=4,'gz'=2] {'gx'}, dimensions={0}, use_global_device_ids=true | all-gather | bytes 81920 | tf_op jit(solution)/shard_map/all_gather | solution.py:76
  80.1 5.9 %collective-permute-start.12 = (bf16[8,1,4,256]{3,2,1,0:T(4,128)(2,1)S(1)}, bf16[8,1,4,256]{3,2,1,0:T(4,128)(2,1)S(1)}, u32[]{:S(2)}, u32[]{:S(2)}) collective-permute-start(bf16[8,1,4,256]{3,2,1,0:T(4,128)(2,1)S(1)} %get-tuple-element.178), channel_id=1, source_target_pairs={{0,2},{2,4},{4,6},{1,3},{3,5},{5,7},{8,10},{10,12},{12,14},{9,11},... | collective-permute-start | bytes 49160 | tf_op jit(solution)/shard_map/ppermute | solution.py:15
  86.0 2.1 collective-permute-start.13
  88.2 3.1 %collective-permute-done.13 = bf16[8,1,4,256]{3,2,1,0:T(4,128)(2,1)S(1)} collective-permute-done((bf16[8,1,4,256]{3,2,1,0:T(4,128)(2,1)S(1)}, bf16[8,1,4,256]{3,2,1,0:T(4,128)(2,1)S(1)}, u32[]{:S(2)}, u32[]{:S(2)}) %collective-permute-start.13) | collective-permute-done | bytes 16416 | tf_op jit(solution)/shard_map/ppermute | solution.py:17
  91.5 1.4 collective-permute-start.14
  92.9 4.0 %collective-permute-start.15 = (bf16[8,6,1,256]{3,2,1,0:T(2,128)(2,1)S(1)}, bf16[8,6,1,256]{3,2,1,0:T(2,128)(2,1)S(1)}, u32[]{:S(2)}, u32[]{:S(2)}) collective-permute-start(bf16[8,6,1,256]{3,2,1,0:T(2,128)(2,1)S(1)} %get-tuple-element.169), channel_id=1, source_target_pairs={{1,0},{3,2},{5,4},{7,6},{9,8},{11,10},{13,12},{15,14},{17,16},{19,... | collective-permute-start | bytes 73736 | tf_op jit(solution)/shard_map/ppermute | solution.py:17
  101.6 1.3 pad_maximum_fusion.34
  112.6 8.5 %all_gather.7 = bf16[8,4,4,512]{3,2,1,0:T(4,128)(2,1)S(1)} all-gather(bf16[8,4,4,128]{3,2,1,0:T(4,128)(2,1)S(1)} %bitcast.716), channel_id=1, replica_groups=mesh['gx'=4,'gy'=4,'gz'=2] {'gx'}, dimensions={3}, use_global_device_ids=true | all-gather | bytes 163840 | tf_op jit(solution)/shard_map/all_gather | solution.py:79
  121.1 4.8 %collective-permute-start.16 = (bf16[8,1,4,512]{3,2,1,0:T(4,128)(2,1)S(1)}, bf16[8,1,4,512]{3,2,1,0:T(4,128)(2,1)S(1)}, u32[]{:S(2)}, u32[]{:S(2)}) collective-permute-start(bf16[8,1,4,512]{3,2,1,0:T(4,128)(2,1)S(1)} %get-tuple-element.154), channel_id=1, source_target_pairs={{0,2},{2,4},{4,6},{1,3},{3,5},{5,7},{8,10},{10,12},{12,14},{9,11},... | collective-permute-start | bytes 98312 | tf_op jit(solution)/shard_map/ppermute | solution.py:15
  125.9 1.9 collective-permute-start.17
  127.9 3.3 %collective-permute-done.17 = bf16[8,1,4,512]{3,2,1,0:T(4,128)(2,1)S(1)} collective-permute-done((bf16[8,1,4,512]{3,2,1,0:T(4,128)(2,1)S(1)}, bf16[8,1,4,512]{3,2,1,0:T(4,128)(2,1)S(1)}, u32[]{:S(2)}, u32[]{:S(2)}) %collective-permute-start.17) | collective-permute-done | bytes 32800 | tf_op jit(solution)/shard_map/ppermute | solution.py:17
  131.5 1.3 collective-permute-start.18
  132.8 4.0 %collective-permute-start.19 = (bf16[8,6,1,512]{3,2,1,0:T(2,128)(2,1)S(1)}, bf16[8,6,1,512]{3,2,1,0:T(2,128)(2,1)S(1)}, u32[]{:S(2)}, u32[]{:S(2)}) collective-permute-start(bf16[8,6,1,512]{3,2,1,0:T(2,128)(2,1)S(1)} %get-tuple-element.143), channel_id=1, source_target_pairs={{1,0},{3,2},{5,4},{7,6},{9,8},{11,10},{13,12},{15,14},{17,16},{19,... | collective-permute-start | bytes 147464 | tf_op jit(solution)/shard_map/ppermute | solution.py:17
  136.8 1.7 fusion.151
  140.2 1.3 fusion.386
  141.5 1.7 fusion.169
  143.5 2.6 %pad_maximum_fusion.20 = (bf16[8,4,4,512]{3,2,1,0:T(4,128)(2,1)S(1)}, bf16[8,4,4,512]{3,2,1,0:T(4,128)(2,1)}, bf16[8,4,4,512]{3,2,1,0:T(4,128)(2,1)S(1)}, bf16[8...) fusion(bf16[8,6,4,512]{3,2,1,0:T(4,128)(2,1)S(1)} %constant_dynamic-update-slice, ...), kind=kLoop, calls=%fused_computation.288 | loop fusion | flops 1572864 | bytes 1081344 | tf_op jit(solution)/shard_map/concatenate | solution.py:13
  148.0 1.7 fusion.157
  152.4 1.1 convolution_add_fusion.74
  153.5 1.1 convolution_add_fusion.73
  154.6 1.1 convolution_add_fusion.72
  155.7 1.1 convolution_add_fusion.71
  156.8 1.1 convolution_add_fusion.70
  157.9 1.1 convolution_add_fusion.69
  162.3 1.1 fusion.35
  166.6 1.1 fusion.38
  175.3 1.1 fusion.41
  176.4 6.9 %all_to_all.15 = bf16[8,4,4,128]{3,2,1,0:T(4,128)(2,1)S(1)} all-to-all(bf16[8,4,4,128]{3,2,1,0:T(4,128)(2,1)S(1)} %bitcast.718), channel_id=1, replica_groups=mesh['gx'=4,'gy'=4,'gz'=2] {'gx'}, dimensions={0} | all-to-all | bytes 65536 | tf_op jit(solution)/shard_map/all_to_all | solution.py:82
  183.8 2.4 %collective-permute-start.20 = (bf16[1,8,8,768]{3,2,1,0:T(8,128)(2,1)S(1)}, bf16[1,8,8,768]{3,2,1,0:T(8,128)(2,1)S(1)}, u32[]{:S(2)}, u32[]{:S(2)}) collective-permute-start(bf16[1,8,8,768]{3,2,1,0:T(8,128)(2,1)S(1)} %get-tuple-element.95), channel_id=1, source_target_pairs={{0,8},{8,16},{16,24},{1,9},{9,17},{17,25},{2,10},{10,18},{18,26},{... | collective-permute-start | bytes 294920 | tf_op jit(solution)/shard_map/ppermute | solution.py:15
  186.1 1.3 collective-permute-start.21
  187.4 1.3 fusion.53
  188.7 3.8 %collective-permute-done.21 = bf16[1,8,8,768]{3,2,1,0:T(8,128)(2,1)S(1)} collective-permute-done((bf16[1,8,8,768]{3,2,1,0:T(8,128)(2,1)S(1)}, bf16[1,8,8,768]{3,2,1,0:T(8,128)(2,1)S(1)}, u32[]{:S(2)}, u32[]{:S(2)}) %collective-permute-start.21) | collective-permute-done | bytes 98336 | tf_op jit(solution)/shard_map/ppermute | solution.py:17
  192.6 1.3 fusion.94
  193.9 4.0 %collective-permute-start.22 = (bf16[6,1,8,768]{3,2,1,0:T(8,128)(2,1)S(1)}, bf16[6,1,8,768]{3,2,1,0:T(8,128)(2,1)S(1)}, u32[]{:S(2)}, u32[]{:S(2)}) collective-permute-start(bf16[6,1,8,768]{3,2,1,0:T(8,128)(2,1)S(1)} %get-tuple-element.68), channel_id=1, source_target_pairs={{0,2},{2,4},{4,6},{1,3},{3,5},{5,7},{8,10},{10,12},{12,14},{9,11},... | collective-permute-start | bytes 221192 | tf_op jit(solution)/shard_map/ppermute | solution.py:15
  197.9 1.9 collective-permute-start.23
  199.8 1.3 fusion.64
  201.1 2.5 %collective-permute-done.23 = bf16[6,1,8,768]{3,2,1,0:T(8,128)(2,1)S(1)} collective-permute-done((bf16[6,1,8,768]{3,2,1,0:T(8,128)(2,1)S(1)}, bf16[6,1,8,768]{3,2,1,0:T(8,128)(2,1)S(1)}, u32[]{:S(2)}, u32[]{:S(2)}) %collective-permute-start.23) | collective-permute-done | bytes 73760 | tf_op jit(solution)/shard_map/ppermute | solution.py:17
  203.8 1.3 collective-permute-start.24
  205.1 4.2 %collective-permute-start.25 = (bf16[6,10,1,768]{3,2,1,0:T(2,128)(2,1)S(1)}, bf16[6,10,1,768]{3,2,1,0:T(2,128)(2,1)S(1)}, u32[]{:S(2)}, u32[]{:S(2)}) collective-permute-start(bf16[6,10,1,768]{3,2,1,0:T(2,128)(2,1)S(1)} %get-tuple-element.43), channel_id=1, source_target_pairs={{1,0},{3,2},{5,4},{7,6},{9,8},{11,10},{13,12},{15,14},{17,16},{19,... | collective-permute-start | bytes 276488 | tf_op jit(solution)/shard_map/ppermute | solution.py:17
  209.6 1.4 fusion.100
  211.1 1.3 fusion.88
  212.4 1.4 fusion.83
  213.8 1.3 fusion.74
  215.1 1.3 fusion.69
  216.4 1.3 fusion.58
  217.7 1.4 pad_maximum_fusion
  (263 shorter events, 61.0 us)
Async XLA Ops:
  0.9 4.5 %collective-permute-start = (bf16[1,16,16,128]{3,2,1,0:T(8,128)(2,1)S(1)}, bf16[1,16,16,128]{3,2,1,0:T(8,128)(2,1)S(1)}, u32[]{:S(2)}, u32[]{:S(2)}) collective-permute-start(bf16[1,16,16,128]{3,2,1,0:T(8,128)(2,1)S(1)} %get-tuple-element.74), channel_id=1, source_target_pairs={{0,8},{8,16},{16,24},{1,9},{9,17},{17,25},{2,10},{10,18},{18,26},{... | collective-permute-start | bytes 196616 | tf_op jit(solution)/shard_map/ppermute | solution.py:15
  4.1 5.0 %collective-permute-start.1 = (bf16[1,16,16,128]{3,2,1,0:T(8,128)(2,1)S(1)}, bf16[1,16,16,128]{3,2,1,0:T(8,128)(2,1)S(1)}, u32[]{:S(2)}, u32[]{:S(2)}) collective-permute-start(bf16[1,16,16,128]{3,2,1,0:T(8,128)(2,1)S(1)} %get-tuple-element.73), channel_id=1, source_target_pairs={{8,0},{16,8},{24,16},{9,1},{17,9},{25,17},{10,2},{18,10},{26,18},{... | collective-permute-start | bytes 196616 | tf_op jit(solution)/shard_map/ppermute | solution.py:17
  11.0 7.1 %collective-permute-start.2 = (bf16[10,1,16,128]{3,2,1,0:T(8,128)(2,1)S(1)}, bf16[10,1,16,128]{3,2,1,0:T(8,128)(2,1)S(1)}, u32[]{:S(2)}, u32[]{:S(2)}) collective-permute-start(bf16[10,1,16,128]{3,2,1,0:T(8,128)(2,1)S(1)} %get-tuple-element.64), channel_id=1, source_target_pairs={{0,2},{2,4},{4,6},{1,3},{3,5},{5,7},{8,10},{10,12},{12,14},{9,11},... | collective-permute-start | bytes 122888 | tf_op jit(solution)/shard_map/ppermute | solution.py:15
  16.1 5.3 %collective-permute-start.3 = (bf16[10,1,16,128]{3,2,1,0:T(8,128)(2,1)S(1)}, bf16[10,1,16,128]{3,2,1,0:T(8,128)(2,1)S(1)}, u32[]{:S(2)}, u32[]{:S(2)}) collective-permute-start(bf16[10,1,16,128]{3,2,1,0:T(8,128)(2,1)S(1)} %get-tuple-element.65), channel_id=1, source_target_pairs={{2,0},{4,2},{6,4},{3,1},{5,3},{7,5},{10,8},{12,10},{14,12},{11,9},... | collective-permute-start | bytes 122888 | tf_op jit(solution)/shard_map/ppermute | solution.py:17
  21.6 6.0 %collective-permute-start.4 = (bf16[10,18,1,128]{3,2,1,0:T(2,128)(2,1)S(1)}, bf16[10,18,1,128]{3,2,1,0:T(2,128)(2,1)S(1)}, u32[]{:S(2)}, u32[]{:S(2)}) collective-permute-start(bf16[10,18,1,128]{3,2,1,0:T(2,128)(2,1)S(1)} %get-tuple-element.47), channel_id=1, source_target_pairs={{0,1},{2,3},{4,5},{6,7},{8,9},{10,11},{12,13},{14,15},{16,17},{18,... | collective-permute-start | bytes 138248 | tf_op jit(solution)/shard_map/ppermute | solution.py:15
  22.9 4.4 %copy-start.3 = (bf16[3,3,3,128,128]{4,3,2,1,0:T(8,128)(2,1)S(1)}, bf16[3,3,3,128,128]{4,3,2,1,0:T(8,128)(2,1)}, u32[]{:S(2)}) copy-start(bf16[3,3,3,128,128]{4,3,2,1,0:T(8,128)(2,1)} %param.7) | copy-start | bytes 2654212
  22.9 5.7 %collective-permute-start.5 = (bf16[10,18,1,128]{3,2,1,0:T(2,128)(2,1)S(1)}, bf16[10,18,1,128]{3,2,1,0:T(2,128)(2,1)S(1)}, u32[]{:S(2)}, u32[]{:S(2)}) collective-permute-start(bf16[10,18,1,128]{3,2,1,0:T(2,128)(2,1)S(1)} %get-tuple-element.48), channel_id=1, source_target_pairs={{1,0},{3,2},{5,4},{7,6},{9,8},{11,10},{13,12},{15,14},{17,16},{19,... | collective-permute-start | bytes 138248 | tf_op jit(solution)/shard_map/ppermute | solution.py:17
  36.1 1.0 copy-start
  40.0 23.7 %copy-start.1 = (bf16[3,3,3,128,256]{4,3,2,1,0:T(8,128)(2,1)S(1)}, bf16[3,3,3,128,256]{4,3,2,1,0:T(8,128)(2,1)}, u32[]{:S(2)}) copy-start(bf16[3,3,3,128,256]{4,3,2,1,0:T(8,128)(2,1)} %param.8) | copy-start | bytes 5308420
  41.0 4.5 %collective-permute-start.6 = (bf16[1,8,8,128]{3,2,1,0:T(8,128)(2,1)S(1)}, bf16[1,8,8,128]{3,2,1,0:T(8,128)(2,1)S(1)}, u32[]{:S(2)}, u32[]{:S(2)}) collective-permute-start(bf16[1,8,8,128]{3,2,1,0:T(8,128)(2,1)S(1)} %get-tuple-element.181), channel_id=1, source_target_pairs={{0,8},{8,16},{16,24},{1,9},{9,17},{17,25},{2,10},{10,18},{18,26},{... | collective-permute-start | bytes 49160 | tf_op jit(solution)/shard_map/ppermute | solution.py:15
  44.2 4.5 %collective-permute-start.7 = (bf16[1,8,8,128]{3,2,1,0:T(8,128)(2,1)S(1)}, bf16[1,8,8,128]{3,2,1,0:T(8,128)(2,1)S(1)}, u32[]{:S(2)}, u32[]{:S(2)}) collective-permute-start(bf16[1,8,8,128]{3,2,1,0:T(8,128)(2,1)S(1)} %get-tuple-element.182), channel_id=1, source_target_pairs={{8,0},{16,8},{24,16},{9,1},{17,9},{25,17},{10,2},{18,10},{26,18},{... | collective-permute-start | bytes 49160 | tf_op jit(solution)/shard_map/ppermute | solution.py:17
  48.7 6.4 %collective-permute-start.8 = (bf16[6,1,8,128]{3,2,1,0:T(8,128)(2,1)S(1)}, bf16[6,1,8,128]{3,2,1,0:T(8,128)(2,1)S(1)}, u32[]{:S(2)}, u32[]{:S(2)}) collective-permute-start(bf16[6,1,8,128]{3,2,1,0:T(8,128)(2,1)S(1)} %get-tuple-element.172), channel_id=1, source_target_pairs={{0,2},{2,4},{4,6},{1,3},{3,5},{5,7},{8,10},{10,12},{12,14},{9,11},... | collective-permute-start | bytes 36872 | tf_op jit(solution)/shard_map/ppermute | solution.py:15
  53.2 5.0 %collective-permute-start.9 = (bf16[6,1,8,128]{3,2,1,0:T(8,128)(2,1)S(1)}, bf16[6,1,8,128]{3,2,1,0:T(8,128)(2,1)S(1)}, u32[]{:S(2)}, u32[]{:S(2)}) collective-permute-start(bf16[6,1,8,128]{3,2,1,0:T(8,128)(2,1)S(1)} %get-tuple-element.173), channel_id=1, source_target_pairs={{2,0},{4,2},{6,4},{3,1},{5,3},{7,5},{10,8},{12,10},{14,12},{11,9},... | collective-permute-start | bytes 36872 | tf_op jit(solution)/shard_map/ppermute | solution.py:17
  58.3 5.6 %collective-permute-start.10 = (bf16[6,10,1,128]{3,2,1,0:T(2,128)(2,1)S(1)}, bf16[6,10,1,128]{3,2,1,0:T(2,128)(2,1)S(1)}, u32[]{:S(2)}, u32[]{:S(2)}) collective-permute-start(bf16[6,10,1,128]{3,2,1,0:T(2,128)(2,1)S(1)} %get-tuple-element.157), channel_id=1, source_target_pairs={{0,1},{2,3},{4,5},{6,7},{8,9},{10,11},{12,13},{14,15},{16,17},{18,... | collective-permute-start | bytes 46088 | tf_op jit(solution)/shard_map/ppermute | solution.py:15
  59.6 5.0 %collective-permute-start.11 = (bf16[6,10,1,128]{3,2,1,0:T(2,128)(2,1)S(1)}, bf16[6,10,1,128]{3,2,1,0:T(2,128)(2,1)S(1)}, u32[]{:S(2)}, u32[]{:S(2)}) collective-permute-start(bf16[6,10,1,128]{3,2,1,0:T(2,128)(2,1)S(1)} %get-tuple-element.158), channel_id=1, source_target_pairs={{1,0},{3,2},{5,4},{7,6},{9,8},{11,10},{13,12},{15,14},{17,16},{19,... | collective-permute-start | bytes 46088 | tf_op jit(solution)/shard_map/ppermute | solution.py:17
  80.1 8.0 %collective-permute-start.12 = (bf16[8,1,4,256]{3,2,1,0:T(4,128)(2,1)S(1)}, bf16[8,1,4,256]{3,2,1,0:T(4,128)(2,1)S(1)}, u32[]{:S(2)}, u32[]{:S(2)}) collective-permute-start(bf16[8,1,4,256]{3,2,1,0:T(4,128)(2,1)S(1)} %get-tuple-element.178), channel_id=1, source_target_pairs={{0,2},{2,4},{4,6},{1,3},{3,5},{5,7},{8,10},{10,12},{12,14},{9,11},... | collective-permute-start | bytes 49160 | tf_op jit(solution)/shard_map/ppermute | solution.py:15
  86.0 5.2 %collective-permute-start.13 = (bf16[8,1,4,256]{3,2,1,0:T(4,128)(2,1)S(1)}, bf16[8,1,4,256]{3,2,1,0:T(4,128)(2,1)S(1)}, u32[]{:S(2)}, u32[]{:S(2)}) collective-permute-start(bf16[8,1,4,256]{3,2,1,0:T(4,128)(2,1)S(1)} %get-tuple-element.177), channel_id=1, source_target_pairs={{2,0},{4,2},{6,4},{3,1},{5,3},{7,5},{10,8},{12,10},{14,12},{11,9},... | collective-permute-start | bytes 49160 | tf_op jit(solution)/shard_map/ppermute | solution.py:17
  91.4 7.4 %copy-start.2 = (bf16[3,3,3,256,128]{4,3,2,1,0:T(8,128)(2,1)S(1)}, bf16[3,3,3,256,128]{4,3,2,1,0:T(8,128)(2,1)}, u32[]{:S(2)}) copy-start(bf16[3,3,3,256,128]{4,3,2,1,0:T(8,128)(2,1)} %param.9) | copy-start | bytes 5308420
  91.5 6.5 %collective-permute-start.14 = (bf16[8,6,1,256]{3,2,1,0:T(2,128)(2,1)S(1)}, bf16[8,6,1,256]{3,2,1,0:T(2,128)(2,1)S(1)}, u32[]{:S(2)}, u32[]{:S(2)}) collective-permute-start(bf16[8,6,1,256]{3,2,1,0:T(2,128)(2,1)S(1)} %get-tuple-element.168), channel_id=1, source_target_pairs={{0,1},{2,3},{4,5},{6,7},{8,9},{10,11},{12,13},{14,15},{16,17},{18,... | collective-permute-start | bytes 73736 | tf_op jit(solution)/shard_map/ppermute | solution.py:15
  92.9 5.2 %collective-permute-start.15 = (bf16[8,6,1,256]{3,2,1,0:T(2,128)(2,1)S(1)}, bf16[8,6,1,256]{3,2,1,0:T(2,128)(2,1)S(1)}, u32[]{:S(2)}, u32[]{:S(2)}) collective-permute-start(bf16[8,6,1,256]{3,2,1,0:T(2,128)(2,1)S(1)} %get-tuple-element.169), channel_id=1, source_target_pairs={{1,0},{3,2},{5,4},{7,6},{9,8},{11,10},{13,12},{15,14},{17,16},{19,... | collective-permute-start | bytes 73736 | tf_op jit(solution)/shard_map/ppermute | solution.py:17
  98.0 3.5 %copy-start.10 = (bf16[8,6,1,256]{3,2,1,0:T(2,128)(2,1)}, bf16[8,6,1,256]{3,2,1,0:T(2,128)(2,1)S(1)}, u32[]{:S(2)}) copy-start(bf16[8,6,1,256]{3,2,1,0:T(2,128)(2,1)S(1)} %collective-permute-done.15) | copy-start | bytes 73732
  104.9 5.9 %copy-start.9 = (bf16[128,256]{1,0:T(8,128)(2,1)S(1)}, bf16[128,256]{1,0:T(8,128)(2,1)}, u32[]{:S(2)}) copy-start(bf16[128,256]{1,0:T(8,128)(2,1)} %reshape.502) | copy-start | bytes 196612
  121.1 6.7 %collective-permute-start.16 = (bf16[8,1,4,512]{3,2,1,0:T(4,128)(2,1)S(1)}, bf16[8,1,4,512]{3,2,1,0:T(4,128)(2,1)S(1)}, u32[]{:S(2)}, u32[]{:S(2)}) collective-permute-start(bf16[8,1,4,512]{3,2,1,0:T(4,128)(2,1)S(1)} %get-tuple-element.154), channel_id=1, source_target_pairs={{0,2},{2,4},{4,6},{1,3},{3,5},{5,7},{8,10},{10,12},{12,14},{9,11},... | collective-permute-start | bytes 98312 | tf_op jit(solution)/shard_map/ppermute | solution.py:15
  125.9 5.2 %collective-permute-start.17 = (bf16[8,1,4,512]{3,2,1,0:T(4,128)(2,1)S(1)}, bf16[8,1,4,512]{3,2,1,0:T(4,128)(2,1)S(1)}, u32[]{:S(2)}, u32[]{:S(2)}) collective-permute-start(bf16[8,1,4,512]{3,2,1,0:T(4,128)(2,1)S(1)} %get-tuple-element.153), channel_id=1, source_target_pairs={{2,0},{4,2},{6,4},{3,1},{5,3},{7,5},{10,8},{12,10},{14,12},{11,9},... | collective-permute-start | bytes 98312 | tf_op jit(solution)/shard_map/ppermute | solution.py:17
  131.5 7.1 %collective-permute-start.18 = (bf16[8,6,1,512]{3,2,1,0:T(2,128)(2,1)S(1)}, bf16[8,6,1,512]{3,2,1,0:T(2,128)(2,1)S(1)}, u32[]{:S(2)}, u32[]{:S(2)}) collective-permute-start(bf16[8,6,1,512]{3,2,1,0:T(2,128)(2,1)S(1)} %get-tuple-element.142), channel_id=1, source_target_pairs={{0,1},{2,3},{4,5},{6,7},{8,9},{10,11},{12,13},{14,15},{16,17},{18,... | collective-permute-start | bytes 147464 | tf_op jit(solution)/shard_map/ppermute | solution.py:15
  132.8 5.8 %collective-permute-start.19 = (bf16[8,6,1,512]{3,2,1,0:T(2,128)(2,1)S(1)}, bf16[8,6,1,512]{3,2,1,0:T(2,128)(2,1)S(1)}, u32[]{:S(2)}, u32[]{:S(2)}) collective-permute-start(bf16[8,6,1,512]{3,2,1,0:T(2,128)(2,1)S(1)} %get-tuple-element.143), channel_id=1, source_target_pairs={{1,0},{3,2},{5,4},{7,6},{9,8},{11,10},{13,12},{15,14},{17,16},{19,... | collective-permute-start | bytes 147464 | tf_op jit(solution)/shard_map/ppermute | solution.py:17
  138.6 0.7 copy-start.4
  139.2 0.6 copy-start.5
  149.8 2.6 %copy-start.8 = (f32[128,128]{1,0:T(8,128)S(1)}, f32[128,128]{1,0:T(8,128)}, u32[]{:S(2)}) copy-start(f32[128,128]{1,0:T(8,128)} %fusion.169) | copy-start | bytes 196612
  152.4 9.9 %copy-start.7 = (f32[128,128]{1,0:T(8,128)S(1)}, f32[128,128]{1,0:T(8,128)}, u32[]{:S(2)}) copy-start(f32[128,128]{1,0:T(8,128)} %fusion.157) | copy-start | bytes 196612
  156.8 9.8 %copy-start.6 = (f32[128,128]{1,0:T(8,128)S(1)}, f32[128,128]{1,0:T(8,128)}, u32[]{:S(2)}) copy-start(f32[128,128]{1,0:T(8,128)} %fusion.151) | copy-start | bytes 196612
  183.8 5.0 %collective-permute-start.20 = (bf16[1,8,8,768]{3,2,1,0:T(8,128)(2,1)S(1)}, bf16[1,8,8,768]{3,2,1,0:T(8,128)(2,1)S(1)}, u32[]{:S(2)}, u32[]{:S(2)}) collective-permute-start(bf16[1,8,8,768]{3,2,1,0:T(8,128)(2,1)S(1)} %get-tuple-element.95), channel_id=1, source_target_pairs={{0,8},{8,16},{16,24},{1,9},{9,17},{17,25},{2,10},{10,18},{18,26},{... | collective-permute-start | bytes 294920 | tf_op jit(solution)/shard_map/ppermute | solution.py:15
  186.1 6.4 %collective-permute-start.21 = (bf16[1,8,8,768]{3,2,1,0:T(8,128)(2,1)S(1)}, bf16[1,8,8,768]{3,2,1,0:T(8,128)(2,1)S(1)}, u32[]{:S(2)}, u32[]{:S(2)}) collective-permute-start(bf16[1,8,8,768]{3,2,1,0:T(8,128)(2,1)S(1)} %get-tuple-element.96), channel_id=1, source_target_pairs={{8,0},{16,8},{24,16},{9,1},{17,9},{25,17},{10,2},{18,10},{26,18},{... | collective-permute-start | bytes 294920 | tf_op jit(solution)/shard_map/ppermute | solution.py:17
  193.9 7.3 %collective-permute-start.22 = (bf16[6,1,8,768]{3,2,1,0:T(8,128)(2,1)S(1)}, bf16[6,1,8,768]{3,2,1,0:T(8,128)(2,1)S(1)}, u32[]{:S(2)}, u32[]{:S(2)}) collective-permute-start(bf16[6,1,8,768]{3,2,1,0:T(8,128)(2,1)S(1)} %get-tuple-element.68), channel_id=1, source_target_pairs={{0,2},{2,4},{4,6},{1,3},{3,5},{5,7},{8,10},{10,12},{12,14},{9,11},... | collective-permute-start | bytes 221192 | tf_op jit(solution)/shard_map/ppermute | solution.py:15
  197.9 5.7 %collective-permute-start.23 = (bf16[6,1,8,768]{3,2,1,0:T(8,128)(2,1)S(1)}, bf16[6,1,8,768]{3,2,1,0:T(8,128)(2,1)S(1)}, u32[]{:S(2)}, u32[]{:S(2)}) collective-permute-start(bf16[6,1,8,768]{3,2,1,0:T(8,128)(2,1)S(1)} %get-tuple-element.69), channel_id=1, source_target_pairs={{2,0},{4,2},{6,4},{3,1},{5,3},{7,5},{10,8},{12,10},{14,12},{11,9},... | collective-permute-start | bytes 221192 | tf_op jit(solution)/shard_map/ppermute | solution.py:17
  203.8 13.8 %collective-permute-start.24 = (bf16[6,10,1,768]{3,2,1,0:T(2,128)(2,1)S(1)}, bf16[6,10,1,768]{3,2,1,0:T(2,128)(2,1)S(1)}, u32[]{:S(2)}, u32[]{:S(2)}) collective-permute-start(bf16[6,10,1,768]{3,2,1,0:T(2,128)(2,1)S(1)} %get-tuple-element.44), channel_id=1, source_target_pairs={{0,1},{2,3},{4,5},{6,7},{8,9},{10,11},{12,13},{14,15},{16,17},{18,... | collective-permute-start | bytes 276488 | tf_op jit(solution)/shard_map/ppermute | solution.py:15
  205.1 12.5 %collective-permute-start.25 = (bf16[6,10,1,768]{3,2,1,0:T(2,128)(2,1)S(1)}, bf16[6,10,1,768]{3,2,1,0:T(2,128)(2,1)S(1)}, u32[]{:S(2)}, u32[]{:S(2)}) collective-permute-start(bf16[6,10,1,768]{3,2,1,0:T(2,128)(2,1)S(1)} %get-tuple-element.43), channel_id=1, source_target_pairs={{1,0},{3,2},{5,4},{7,6},{9,8},{11,10},{13,12},{15,14},{17,16},{19,... | collective-permute-start | bytes 276488 | tf_op jit(solution)/shard_map/ppermute | solution.py:17
  209.5 9.9 %slice-start = ((s8[10616832]{0:T(1024)(128)(4,1)}), s8[4194304]{0:T(1024)(128)(4,1)S(1)}, s32[]{:S(2)}) async-start(s8[10616832]{0:T(1024)(128)(4,1)} %bitcast.627), calls=%async_computation.1 | async-start | bytes 8388608
  212.4 7.0 %slice-start.1 = ((s8[10616832]{0:T(1024)(128)(4,1)}), s8[4194304]{0:T(1024)(128)(4,1)S(1)}, s32[]{:S(2)}) async-start(s8[10616832]{0:T(1024)(128)(4,1)} %bitcast.627), calls=%async_computation.2 | async-start | bytes 8388608
  217.7 1.8 slice-start.2
where the time goes:
time: 228 us; the launch traced here: 226 us
  starting transfers between devices  73.7 us (32%)
  matrix products  69.5 us (30%)
  waiting for transfers between devices  27.9 us (12%)
  blocking collectives  25.6 us (11%)
  local copies, waits for them, and re-layouts  16.5 us (7%)
  other arithmetic  10.6 us (5%)
    dot_general x135, matrix products, convolve(): jnp.dot(window.reshape(-1, channels), kernel[offset_x, offset_y, offset_z...  69.5 us
    ppermute x13, starting transfers between devices, with_halo(): lax.ppermute(tail, axis, [(i, (i + 1) % count) for i in range(ends)])  39.6 us
    ppermute x13, starting transfers between devices, with_halo(): lax.ppermute(head, axis, [((i + 1) % count, i) for i in range(ends)])  34 us
    ppermute x13, waiting for transfers between devices, with_halo(): lax.ppermute(head, axis, [((i + 1) % count, i) for i in range(ends)])  27.8 us
    all_gather x1, blocking collectives, on_device(): column = lax.all_gather(coarse, 'gx', axis=0, tiled=True)  10.3 us
    concatenate x16, other arithmetic, with_halo(): jnp.concatenate([lax.ppermute(tail, axis, [(i, (i + 1) % count) for i in...  9.53 us
    all_gather x1, blocking collectives, on_device(): filters = lax.all_gather(bottom_first, 'gx', axis=3, tiled=True)  8.49 us
    reshape x54, local copies, waits for them, and re-layouts, convolve(): window.reshape(-1, channels)  7.16 us
  transfers between devices with their start and end apart: 26, of which 11 were waited for; matrix products, arithmetic and copies ran while one was open for 6% of the time, Pallas kernels for 0%

commit v1 on v0

--- a/solution.py
+++ b/solution.py
@@ -79,7 +79,12 @@
     filters = lax.all_gather(bottom_first, "gx", axis=3, tiled=True)
     filters = with_halo(filters, (("gy", 1), ("gz", 2)), 1)
     bottom_second = rectify(convolve(pad_first(filters), w_bottom_out))
-    regrouped = lax.all_to_all(bottom_second, "gx", split_axis=0, concat_axis=3, tiled=True)
+    regrouped = jnp.concatenate(
+        lax.all_to_all(
+            jnp.stack(jnp.split(bottom_second, lax.axis_size("gx"), axis=0)), "gx", 0, 0
+        ),
+        axis=3,
+    )
     joined = jnp.concatenate([enlarge(regrouped), skip_level], axis=3)
     joined = with_halo(joined, (("gx", 0), ("gy", 1), ("gz", 2)), 1)
     return convolve(joined, w_up).astype(jnp.bfloat16)

time: 228 us -> 228 us (level)
  no operation moved by 1% of the time
where the time goes in v1:
time: 228 us; the launch traced here: 226 us
  starting transfers between devices  73.6 us (32%)
  matrix products  69.5 us (30%)
  waiting for transfers between devices  27.9 us (12%)
  blocking collectives  25.6 us (11%)
  local copies, waits for them, and re-layouts  16.4 us (7%)
  other arithmetic  10.6 us (5%)
    dot_general x135, matrix products, convolve(): jnp.dot(window.reshape(-1, channels), kernel[offset_x, offset_y, offset_z...  69.5 us
    ppermute x13, starting transfers between devices, with_halo(): lax.ppermute(tail, axis, [(i, (i + 1) % count) for i in range(ends)])  39.6 us
    ppermute x13, starting transfers between devices, with_halo(): lax.ppermute(head, axis, [((i + 1) % count, i) for i in range(ends)])  34 us
    ppermute x13, waiting for transfers between devices, with_halo(): lax.ppermute(head, axis, [((i + 1) % count, i) for i in range(ends)])  27.8 us
    all_gather x1, blocking collectives, on_device(): column = lax.all_gather(coarse, 'gx', axis=0, tiled=True)  10.3 us
    concatenate x16, other arithmetic, with_halo(): jnp.concatenate([lax.ppermute(tail, axis, [(i, (i + 1) % count) for i in...  9.54 us
    all_gather x1, blocking collectives, on_device(): filters = lax.all_gather(bottom_first, 'gx', axis=3, tiled=True)  8.49 us
    reshape x54, local copies, waits for them, and re-layouts, convolve(): window.reshape(-1, channels)  7.1 us
  transfers between devices with their start and end apart: 26, of which 11 were waited for; matrix products, arithmetic and copies ran while one was open for 6% of the time, Pallas kernels for 0%

profile of v1, /device:TPU:3, one launch (start us, length us, event | category | flops | bytes accessed | tf_op | source)
XLA Modules:
  0.0 225.6 jit_solution(5815712846739366740)
XLA Ops:
  0.9 3.2 %collective-permute-start = (bf16[1,16,16,128]{3,2,1,0:T(8,128)(2,1)S(1)}, bf16[1,16,16,128]{3,2,1,0:T(8,128)(2,1)S(1)}, u32[]{:S(2)}, u32[]{:S(2)}) collective-permute-start(bf16[1,16,16,128]{3,2,1,0:T(8,128)(2,1)S(1)} %get-tuple-element.74), channel_id=1, source_target_pairs={{0,8},{8,16},{16,24},{1,9},{9,17},{17,25},{2,10},{10,18},{18,26},{... | collective-permute-start | bytes 196616 | tf_op jit(solution)/shard_map/ppermute | solution.py:15
  4.1 1.3 collective-permute-start.1
  5.4 3.7 %collective-permute-done.1 = bf16[1,16,16,128]{3,2,1,0:T(8,128)(2,1)S(1)} collective-permute-done((bf16[1,16,16,128]{3,2,1,0:T(8,128)(2,1)S(1)}, bf16[1,16,16,128]{3,2,1,0:T(8,128)(2,1)S(1)}, u32[]{:S(2)}, u32[]{:S(2)}) %collective-permute-start.1) | collective-permute-done | bytes 65568 | tf_op jit(solution)/shard_map/ppermute | solution.py:17
  9.1 1.8 pad_maximum_fusion.4
  11.0 5.1 %collective-permute-start.2 = (bf16[10,1,16,128]{3,2,1,0:T(8,128)(2,1)S(1)}, bf16[10,1,16,128]{3,2,1,0:T(8,128)(2,1)S(1)}, u32[]{:S(2)}, u32[]{:S(2)}) collective-permute-start(bf16[10,1,16,128]{3,2,1,0:T(8,128)(2,1)S(1)} %get-tuple-element.64), channel_id=1, source_target_pairs={{0,2},{2,4},{4,6},{1,3},{3,5},{5,7},{8,10},{10,12},{12,14},{9,11},... | collective-permute-start | bytes 122888 | tf_op jit(solution)/shard_map/ppermute | solution.py:15
  16.1 1.9 collective-permute-start.3
  18.1 3.4 %collective-permute-done.3 = bf16[10,1,16,128]{3,2,1,0:T(8,128)(2,1)S(1)} collective-permute-done((bf16[10,1,16,128]{3,2,1,0:T(8,128)(2,1)S(1)}, bf16[10,1,16,128]{3,2,1,0:T(8,128)(2,1)S(1)}, u32[]{:S(2)}, u32[]{:S(2)}) %collective-permute-start.3) | collective-permute-done | bytes 40992 | tf_op jit(solution)/shard_map/ppermute | solution.py:17
  21.6 1.3 collective-permute-start.4
  22.9 4.1 %collective-permute-start.5 = (bf16[10,18,1,128]{3,2,1,0:T(2,128)(2,1)S(1)}, bf16[10,18,1,128]{3,2,1,0:T(2,128)(2,1)S(1)}, u32[]{:S(2)}, u32[]{:S(2)}) collective-permute-start(bf16[10,18,1,128]{3,2,1,0:T(2,128)(2,1)S(1)} %get-tuple-element.48), channel_id=1, source_target_pairs={{1,0},{3,2},{5,4},{7,6},{9,8},{11,10},{13,12},{15,14},{17,16},{19,... | collective-permute-start | bytes 138248 | tf_op jit(solution)/shard_map/ppermute | solution.py:17
  29.5 2.6 %fusion.380 = (bf16[8,16,16,128]{3,2,1,0:T(8,128)(2,1)S(1)}, bf16[8,16,16,128]{3,2,1,0:T(8,128)(2,1)S(1)}, bf16[8,16,16,128]{3,2,1,0:T(8,128)(2,1)S(1)}, bf16[8,...) fusion(bf16[10,18,17,128]{3,2,1,0:T(8,128)(2,1)S(1)} %get-tuple, ...), kind=kLoop, calls=%fused_computation.567 | loop fusion | bytes 18874368 | tf_op jit(solution)/shard_map/slice | solution.py:33
  41.0 3.2 %collective-permute-start.6 = (bf16[1,8,8,128]{3,2,1,0:T(8,128)(2,1)S(1)}, bf16[1,8,8,128]{3,2,1,0:T(8,128)(2,1)S(1)}, u32[]{:S(2)}, u32[]{:S(2)}) collective-permute-start(bf16[1,8,8,128]{3,2,1,0:T(8,128)(2,1)S(1)} %get-tuple-element.181), channel_id=1, source_target_pairs={{0,8},{8,16},{16,24},{1,9},{9,17},{17,25},{2,10},{10,18},{18,26},{... | collective-permute-start | bytes 49160 | tf_op jit(solution)/shard_map/ppermute | solution.py:15
  44.2 1.3 collective-permute-start.7
  45.6 3.2 %collective-permute-done.7 = bf16[1,8,8,128]{3,2,1,0:T(8,128)(2,1)S(1)} collective-permute-done((bf16[1,8,8,128]{3,2,1,0:T(8,128)(2,1)S(1)}, bf16[1,8,8,128]{3,2,1,0:T(8,128)(2,1)S(1)}, u32[]{:S(2)}, u32[]{:S(2)}) %collective-permute-start.7) | collective-permute-done | bytes 16416 | tf_op jit(solution)/shard_map/ppermute | solution.py:17
  48.7 4.4 %collective-permute-start.8 = (bf16[6,1,8,128]{3,2,1,0:T(8,128)(2,1)S(1)}, bf16[6,1,8,128]{3,2,1,0:T(8,128)(2,1)S(1)}, u32[]{:S(2)}, u32[]{:S(2)}) collective-permute-start(bf16[6,1,8,128]{3,2,1,0:T(8,128)(2,1)S(1)} %get-tuple-element.172), channel_id=1, source_target_pairs={{0,2},{2,4},{4,6},{1,3},{3,5},{5,7},{8,10},{10,12},{12,14},{9,11},... | collective-permute-start | bytes 36872 | tf_op jit(solution)/shard_map/ppermute | solution.py:15
  53.2 1.9 collective-permute-start.9
  55.2 3.1 %collective-permute-done.9 = bf16[6,1,8,128]{3,2,1,0:T(8,128)(2,1)S(1)} collective-permute-done((bf16[6,1,8,128]{3,2,1,0:T(8,128)(2,1)S(1)}, bf16[6,1,8,128]{3,2,1,0:T(8,128)(2,1)S(1)}, u32[]{:S(2)}, u32[]{:S(2)}) %collective-permute-start.9) | collective-permute-done | bytes 12320 | tf_op jit(solution)/shard_map/ppermute | solution.py:17
  58.3 1.3 collective-permute-start.10
  59.6 4.0 %collective-permute-start.11 = (bf16[6,10,1,128]{3,2,1,0:T(2,128)(2,1)S(1)}, bf16[6,10,1,128]{3,2,1,0:T(2,128)(2,1)S(1)}, u32[]{:S(2)}, u32[]{:S(2)}) collective-permute-start(bf16[6,10,1,128]{3,2,1,0:T(2,128)(2,1)S(1)} %get-tuple-element.158), channel_id=1, source_target_pairs={{1,0},{3,2},{5,4},{7,6},{9,8},{11,10},{13,12},{15,14},{17,16},{19,... | collective-permute-start | bytes 46088 | tf_op jit(solution)/shard_map/ppermute | solution.py:17
  69.9 10.3 %all_gather.6 = bf16[8,4,4,256]{3,2,1,0:T(4,128)(2,1)S(1)} all-gather(bf16[2,4,4,256]{3,2,1,0:T(4,128)(2,1)S(1)} %reduce_max.19), channel_id=1, replica_groups=mesh['gx'=4,'gy'=4,'gz'=2] {'gx'}, dimensions={0}, use_global_device_ids=true | all-gather | bytes 81920 | tf_op jit(solution)/shard_map/all_gather | solution.py:76
  80.2 5.9 %collective-permute-start.12 = (bf16[8,1,4,256]{3,2,1,0:T(4,128)(2,1)S(1)}, bf16[8,1,4,256]{3,2,1,0:T(4,128)(2,1)S(1)}, u32[]{:S(2)}, u32[]{:S(2)}) collective-permute-start(bf16[8,1,4,256]{3,2,1,0:T(4,128)(2,1)S(1)} %get-tuple-element.178), channel_id=1, source_target_pairs={{0,2},{2,4},{4,6},{1,3},{3,5},{5,7},{8,10},{10,12},{12,14},{9,11},... | collective-permute-start | bytes 49160 | tf_op jit(solution)/shard_map/ppermute | solution.py:15
  86.1 2.1 collective-permute-start.13
  88.2 3.1 %collective-permute-done.13 = bf16[8,1,4,256]{3,2,1,0:T(4,128)(2,1)S(1)} collective-permute-done((bf16[8,1,4,256]{3,2,1,0:T(4,128)(2,1)S(1)}, bf16[8,1,4,256]{3,2,1,0:T(4,128)(2,1)S(1)}, u32[]{:S(2)}, u32[]{:S(2)}) %collective-permute-start.13) | collective-permute-done | bytes 16416 | tf_op jit(solution)/shard_map/ppermute | solution.py:17
  91.5 1.4 collective-permute-start.14
  92.9 4.0 %collective-permute-start.15 = (bf16[8,6,1,256]{3,2,1,0:T(2,128)(2,1)S(1)}, bf16[8,6,1,256]{3,2,1,0:T(2,128)(2,1)S(1)}, u32[]{:S(2)}, u32[]{:S(2)}) collective-permute-start(bf16[8,6,1,256]{3,2,1,0:T(2,128)(2,1)S(1)} %get-tuple-element.169), channel_id=1, source_target_pairs={{1,0},{3,2},{5,4},{7,6},{9,8},{11,10},{13,12},{15,14},{17,16},{19,... | collective-permute-start | bytes 73736 | tf_op jit(solution)/shard_map/ppermute | solution.py:17
  101.6 1.3 pad_maximum_fusion.34
  112.6 8.5 %all_gather.7 = bf16[8,4,4,512]{3,2,1,0:T(4,128)(2,1)S(1)} all-gather(bf16[8,4,4,128]{3,2,1,0:T(4,128)(2,1)S(1)} %bitcast.722), channel_id=1, replica_groups=mesh['gx'=4,'gy'=4,'gz'=2] {'gx'}, dimensions={3}, use_global_device_ids=true | all-gather | bytes 163840 | tf_op jit(solution)/shard_map/all_gather | solution.py:79
  121.1 4.8 %collective-permute-start.16 = (bf16[8,1,4,512]{3,2,1,0:T(4,128)(2,1)S(1)}, bf16[8,1,4,512]{3,2,1,0:T(4,128)(2,1)S(1)}, u32[]{:S(2)}, u32[]{:S(2)}) collective-permute-start(bf16[8,1,4,512]{3,2,1,0:T(4,128)(2,1)S(1)} %get-tuple-element.154), channel_id=1, source_target_pairs={{0,2},{2,4},{4,6},{1,3},{3,5},{5,7},{8,10},{10,12},{12,14},{9,11},... | collective-permute-start | bytes 98312 | tf_op jit(solution)/shard_map/ppermute | solution.py:15
  125.9 1.9 collective-permute-start.17
  127.8 3.3 %collective-permute-done.17 = bf16[8,1,4,512]{3,2,1,0:T(4,128)(2,1)S(1)} collective-permute-done((bf16[8,1,4,512]{3,2,1,0:T(4,128)(2,1)S(1)}, bf16[8,1,4,512]{3,2,1,0:T(4,128)(2,1)S(1)}, u32[]{:S(2)}, u32[]{:S(2)}) %collective-permute-start.17) | collective-permute-done | bytes 32800 | tf_op jit(solution)/shard_map/ppermute | solution.py:17
  131.5 1.3 collective-permute-start.18
  132.8 4.0 %collective-permute-start.19 = (bf16[8,6,1,512]{3,2,1,0:T(2,128)(2,1)S(1)}, bf16[8,6,1,512]{3,2,1,0:T(2,128)(2,1)S(1)}, u32[]{:S(2)}, u32[]{:S(2)}) collective-permute-start(bf16[8,6,1,512]{3,2,1,0:T(2,128)(2,1)S(1)} %get-tuple-element.143), channel_id=1, source_target_pairs={{1,0},{3,2},{5,4},{7,6},{9,8},{11,10},{13,12},{15,14},{17,16},{19,... | collective-permute-start | bytes 147464 | tf_op jit(solution)/shard_map/ppermute | solution.py:17
  136.8 1.7 fusion.151
  140.2 1.3 fusion.386
  141.5 1.7 fusion.169
  143.5 2.6 %pad_maximum_fusion.20 = (bf16[8,4,4,512]{3,2,1,0:T(4,128)(2,1)S(1)}, bf16[8,4,4,512]{3,2,1,0:T(4,128)(2,1)}, bf16[8,4,4,512]{3,2,1,0:T(4,128)(2,1)S(1)}, bf16[8...) fusion(bf16[8,6,4,512]{3,2,1,0:T(4,128)(2,1)S(1)} %constant_dynamic-update-slice, ...), kind=kLoop, calls=%fused_computation.288 | loop fusion | flops 1572864 | bytes 1081344 | tf_op jit(solution)/shard_map/concatenate | solution.py:13
  147.9 1.7 fusion.157
  152.3 1.1 convolution_add_fusion.74
  153.5 1.1 convolution_add_fusion.73
  154.6 1.1 convolution_add_fusion.72
  155.6 1.1 convolution_add_fusion.71
  156.7 1.1 convolution_add_fusion.70
  162.2 1.1 fusion.35
  166.6 1.1 fusion.38
  167.7 1.1 convolution_add_fusion.60
  175.3 1.1 fusion.41
  176.4 6.9 %all_to_all.5 = bf16[4,2,4,4,128]{4,3,2,1,0:T(4,128)(2,1)S(1)} all-to-all(bf16[4,2,4,4,128]{4,3,2,1,0:T(4,128)(2,1)S(1)} %pad_maximum_fusion.38), channel_id=1, replica_groups=mesh['gx'=4,'gy'=4,'gz'=2] {'gx'}, dimensions={0} | all-to-all | bytes 65536 | tf_op jit(solution)/shard_map/all_to_all | solution.py:83
  183.7 2.4 %collective-permute-start.20 = (bf16[1,8,8,768]{3,2,1,0:T(8,128)(2,1)S(1)}, bf16[1,8,8,768]{3,2,1,0:T(8,128)(2,1)S(1)}, u32[]{:S(2)}, u32[]{:S(2)}) collective-permute-start(bf16[1,8,8,768]{3,2,1,0:T(8,128)(2,1)S(1)} %get-tuple-element.95), channel_id=1, source_target_pairs={{0,8},{8,16},{16,24},{1,9},{9,17},{17,25},{2,10},{10,18},{18,26},{... | collective-permute-start | bytes 294920 | tf_op jit(solution)/shard_map/ppermute | solution.py:15
  186.1 1.3 collective-permute-start.21
  187.4 1.3 fusion.53
  188.7 3.8 %collective-permute-done.21 = bf16[1,8,8,768]{3,2,1,0:T(8,128)(2,1)S(1)} collective-permute-done((bf16[1,8,8,768]{3,2,1,0:T(8,128)(2,1)S(1)}, bf16[1,8,8,768]{3,2,1,0:T(8,128)(2,1)S(1)}, u32[]{:S(2)}, u32[]{:S(2)}) %collective-permute-start.21) | collective-permute-done | bytes 98336 | tf_op jit(solution)/shard_map/ppermute | solution.py:17
  192.5 1.3 fusion.94
  193.8 4.0 %collective-permute-start.22 = (bf16[6,1,8,768]{3,2,1,0:T(8,128)(2,1)S(1)}, bf16[6,1,8,768]{3,2,1,0:T(8,128)(2,1)S(1)}, u32[]{:S(2)}, u32[]{:S(2)}) collective-permute-start(bf16[6,1,8,768]{3,2,1,0:T(8,128)(2,1)S(1)} %get-tuple-element.68), channel_id=1, source_target_pairs={{0,2},{2,4},{4,6},{1,3},{3,5},{5,7},{8,10},{10,12},{12,14},{9,11},... | collective-permute-start | bytes 221192 | tf_op jit(solution)/shard_map/ppermute | solution.py:15
  197.8 1.9 collective-permute-start.23
  199.8 1.3 fusion.64
  201.1 2.5 %collective-permute-done.23 = bf16[6,1,8,768]{3,2,1,0:T(8,128)(2,1)S(1)} collective-permute-done((bf16[6,1,8,768]{3,2,1,0:T(8,128)(2,1)S(1)}, bf16[6,1,8,768]{3,2,1,0:T(8,128)(2,1)S(1)}, u32[]{:S(2)}, u32[]{:S(2)}) %collective-permute-start.23) | collective-permute-done | bytes 73760 | tf_op jit(solution)/shard_map/ppermute | solution.py:17
  203.8 1.3 collective-permute-start.24
  205.1 4.2 %collective-permute-start.25 = (bf16[6,10,1,768]{3,2,1,0:T(2,128)(2,1)S(1)}, bf16[6,10,1,768]{3,2,1,0:T(2,128)(2,1)S(1)}, u32[]{:S(2)}, u32[]{:S(2)}) collective-permute-start(bf16[6,10,1,768]{3,2,1,0:T(2,128)(2,1)S(1)} %get-tuple-element.43), channel_id=1, source_target_pairs={{1,0},{3,2},{5,4},{7,6},{9,8},{11,10},{13,12},{15,14},{17,16},{19,... | collective-permute-start | bytes 276488 | tf_op jit(solution)/shard_map/ppermute | solution.py:17
  209.5 1.4 fusion.100
  211.1 1.3 fusion.88
  212.3 1.4 fusion.83
  213.8 1.3 fusion.74
  215.0 1.3 fusion.69
  216.3 1.3 fusion.58
  217.6 1.4 pad_maximum_fusion
  (263 shorter events, 61.0 us)
Async XLA Ops:
  0.9 4.5 %collective-permute-start = (bf16[1,16,16,128]{3,2,1,0:T(8,128)(2,1)S(1)}, bf16[1,16,16,128]{3,2,1,0:T(8,128)(2,1)S(1)}, u32[]{:S(2)}, u32[]{:S(2)}) collective-permute-start(bf16[1,16,16,128]{3,2,1,0:T(8,128)(2,1)S(1)} %get-tuple-element.74), channel_id=1, source_target_pairs={{0,8},{8,16},{16,24},{1,9},{9,17},{17,25},{2,10},{10,18},{18,26},{... | collective-permute-start | bytes 196616 | tf_op jit(solution)/shard_map/ppermute | solution.py:15
  4.1 5.0 %collective-permute-start.1 = (bf16[1,16,16,128]{3,2,1,0:T(8,128)(2,1)S(1)}, bf16[1,16,16,128]{3,2,1,0:T(8,128)(2,1)S(1)}, u32[]{:S(2)}, u32[]{:S(2)}) collective-permute-start(bf16[1,16,16,128]{3,2,1,0:T(8,128)(2,1)S(1)} %get-tuple-element.73), channel_id=1, source_target_pairs={{8,0},{16,8},{24,16},{9,1},{17,9},{25,17},{10,2},{18,10},{26,18},{... | collective-permute-start | bytes 196616 | tf_op jit(solution)/shard_map/ppermute | solution.py:17
  11.0 7.1 %collective-permute-start.2 = (bf16[10,1,16,128]{3,2,1,0:T(8,128)(2,1)S(1)}, bf16[10,1,16,128]{3,2,1,0:T(8,128)(2,1)S(1)}, u32[]{:S(2)}, u32[]{:S(2)}) collective-permute-start(bf16[10,1,16,128]{3,2,1,0:T(8,128)(2,1)S(1)} %get-tuple-element.64), channel_id=1, source_target_pairs={{0,2},{2,4},{4,6},{1,3},{3,5},{5,7},{8,10},{10,12},{12,14},{9,11},... | collective-permute-start | bytes 122888 | tf_op jit(solution)/shard_map/ppermute | solution.py:15
  16.1 5.3 %collective-permute-start.3 = (bf16[10,1,16,128]{3,2,1,0:T(8,128)(2,1)S(1)}, bf16[10,1,16,128]{3,2,1,0:T(8,128)(2,1)S(1)}, u32[]{:S(2)}, u32[]{:S(2)}) collective-permute-start(bf16[10,1,16,128]{3,2,1,0:T(8,128)(2,1)S(1)} %get-tuple-element.65), channel_id=1, source_target_pairs={{2,0},{4,2},{6,4},{3,1},{5,3},{7,5},{10,8},{12,10},{14,12},{11,9},... | collective-permute-start | bytes 122888 | tf_op jit(solution)/shard_map/ppermute | solution.py:17
  21.6 5.9 %collective-permute-start.4 = (bf16[10,18,1,128]{3,2,1,0:T(2,128)(2,1)S(1)}, bf16[10,18,1,128]{3,2,1,0:T(2,128)(2,1)S(1)}, u32[]{:S(2)}, u32[]{:S(2)}) collective-permute-start(bf16[10,18,1,128]{3,2,1,0:T(2,128)(2,1)S(1)} %get-tuple-element.47), channel_id=1, source_target_pairs={{0,1},{2,3},{4,5},{6,7},{8,9},{10,11},{12,13},{14,15},{16,17},{18,... | collective-permute-start | bytes 138248 | tf_op jit(solution)/shard_map/ppermute | solution.py:15
  22.9 4.4 %copy-start.3 = (bf16[3,3,3,128,128]{4,3,2,1,0:T(8,128)(2,1)S(1)}, bf16[3,3,3,128,128]{4,3,2,1,0:T(8,128)(2,1)}, u32[]{:S(2)}) copy-start(bf16[3,3,3,128,128]{4,3,2,1,0:T(8,128)(2,1)} %param.7) | copy-start | bytes 2654212
  22.9 5.7 %collective-permute-start.5 = (bf16[10,18,1,128]{3,2,1,0:T(2,128)(2,1)S(1)}, bf16[10,18,1,128]{3,2,1,0:T(2,128)(2,1)S(1)}, u32[]{:S(2)}, u32[]{:S(2)}) collective-permute-start(bf16[10,18,1,128]{3,2,1,0:T(2,128)(2,1)S(1)} %get-tuple-element.48), channel_id=1, source_target_pairs={{1,0},{3,2},{5,4},{7,6},{9,8},{11,10},{13,12},{15,14},{17,16},{19,... | collective-permute-start | bytes 138248 | tf_op jit(solution)/shard_map/ppermute | solution.py:17
  36.1 1.0 copy-start
  40.0 23.7 %copy-start.1 = (bf16[3,3,3,128,256]{4,3,2,1,0:T(8,128)(2,1)S(1)}, bf16[3,3,3,128,256]{4,3,2,1,0:T(8,128)(2,1)}, u32[]{:S(2)}) copy-start(bf16[3,3,3,128,256]{4,3,2,1,0:T(8,128)(2,1)} %param.8) | copy-start | bytes 5308420
  41.0 4.5 %collective-permute-start.6 = (bf16[1,8,8,128]{3,2,1,0:T(8,128)(2,1)S(1)}, bf16[1,8,8,128]{3,2,1,0:T(8,128)(2,1)S(1)}, u32[]{:S(2)}, u32[]{:S(2)}) collective-permute-start(bf16[1,8,8,128]{3,2,1,0:T(8,128)(2,1)S(1)} %get-tuple-element.181), channel_id=1, source_target_pairs={{0,8},{8,16},{16,24},{1,9},{9,17},{17,25},{2,10},{10,18},{18,26},{... | collective-permute-start | bytes 49160 | tf_op jit(solution)/shard_map/ppermute | solution.py:15
  44.2 4.5 %collective-permute-start.7 = (bf16[1,8,8,128]{3,2,1,0:T(8,128)(2,1)S(1)}, bf16[1,8,8,128]{3,2,1,0:T(8,128)(2,1)S(1)}, u32[]{:S(2)}, u32[]{:S(2)}) collective-permute-start(bf16[1,8,8,128]{3,2,1,0:T(8,128)(2,1)S(1)} %get-tuple-element.182), channel_id=1, source_target_pairs={{8,0},{16,8},{24,16},{9,1},{17,9},{25,17},{10,2},{18,10},{26,18},{... | collective-permute-start | bytes 49160 | tf_op jit(solution)/shard_map/ppermute | solution.py:17
  48.7 6.4 %collective-permute-start.8 = (bf16[6,1,8,128]{3,2,1,0:T(8,128)(2,1)S(1)}, bf16[6,1,8,128]{3,2,1,0:T(8,128)(2,1)S(1)}, u32[]{:S(2)}, u32[]{:S(2)}) collective-permute-start(bf16[6,1,8,128]{3,2,1,0:T(8,128)(2,1)S(1)} %get-tuple-element.172), channel_id=1, source_target_pairs={{0,2},{2,4},{4,6},{1,3},{3,5},{5,7},{8,10},{10,12},{12,14},{9,11},... | collective-permute-start | bytes 36872 | tf_op jit(solution)/shard_map/ppermute | solution.py:15
  53.2 5.0 %collective-permute-start.9 = (bf16[6,1,8,128]{3,2,1,0:T(8,128)(2,1)S(1)}, bf16[6,1,8,128]{3,2,1,0:T(8,128)(2,1)S(1)}, u32[]{:S(2)}, u32[]{:S(2)}) collective-permute-start(bf16[6,1,8,128]{3,2,1,0:T(8,128)(2,1)S(1)} %get-tuple-element.173), channel_id=1, source_target_pairs={{2,0},{4,2},{6,4},{3,1},{5,3},{7,5},{10,8},{12,10},{14,12},{11,9},... | collective-permute-start | bytes 36872 | tf_op jit(solution)/shard_map/ppermute | solution.py:17
  58.3 5.6 %collective-permute-start.10 = (bf16[6,10,1,128]{3,2,1,0:T(2,128)(2,1)S(1)}, bf16[6,10,1,128]{3,2,1,0:T(2,128)(2,1)S(1)}, u32[]{:S(2)}, u32[]{:S(2)}) collective-permute-start(bf16[6,10,1,128]{3,2,1,0:T(2,128)(2,1)S(1)} %get-tuple-element.157), channel_id=1, source_target_pairs={{0,1},{2,3},{4,5},{6,7},{8,9},{10,11},{12,13},{14,15},{16,17},{18,... | collective-permute-start | bytes 46088 | tf_op jit(solution)/shard_map/ppermute | solution.py:15
  59.6 5.0 %collective-permute-start.11 = (bf16[6,10,1,128]{3,2,1,0:T(2,128)(2,1)S(1)}, bf16[6,10,1,128]{3,2,1,0:T(2,128)(2,1)S(1)}, u32[]{:S(2)}, u32[]{:S(2)}) collective-permute-start(bf16[6,10,1,128]{3,2,1,0:T(2,128)(2,1)S(1)} %get-tuple-element.158), channel_id=1, source_target_pairs={{1,0},{3,2},{5,4},{7,6},{9,8},{11,10},{13,12},{15,14},{17,16},{19,... | collective-permute-start | bytes 46088 | tf_op jit(solution)/shard_map/ppermute | solution.py:17
  80.2 8.0 %collective-permute-start.12 = (bf16[8,1,4,256]{3,2,1,0:T(4,128)(2,1)S(1)}, bf16[8,1,4,256]{3,2,1,0:T(4,128)(2,1)S(1)}, u32[]{:S(2)}, u32[]{:S(2)}) collective-permute-start(bf16[8,1,4,256]{3,2,1,0:T(4,128)(2,1)S(1)} %get-tuple-element.178), channel_id=1, source_target_pairs={{0,2},{2,4},{4,6},{1,3},{3,5},{5,7},{8,10},{10,12},{12,14},{9,11},... | collective-permute-start | bytes 49160 | tf_op jit(solution)/shard_map/ppermute | solution.py:15
  86.1 5.2 %collective-permute-start.13 = (bf16[8,1,4,256]{3,2,1,0:T(4,128)(2,1)S(1)}, bf16[8,1,4,256]{3,2,1,0:T(4,128)(2,1)S(1)}, u32[]{:S(2)}, u32[]{:S(2)}) collective-permute-start(bf16[8,1,4,256]{3,2,1,0:T(4,128)(2,1)S(1)} %get-tuple-element.177), channel_id=1, source_target_pairs={{2,0},{4,2},{6,4},{3,1},{5,3},{7,5},{10,8},{12,10},{14,12},{11,9},... | collective-permute-start | bytes 49160 | tf_op jit(solution)/shard_map/ppermute | solution.py:17
  91.4 7.4 %copy-start.2 = (bf16[3,3,3,256,128]{4,3,2,1,0:T(8,128)(2,1)S(1)}, bf16[3,3,3,256,128]{4,3,2,1,0:T(8,128)(2,1)}, u32[]{:S(2)}) copy-start(bf16[3,3,3,256,128]{4,3,2,1,0:T(8,128)(2,1)} %param.9) | copy-start | bytes 5308420
  91.5 6.5 %collective-permute-start.14 = (bf16[8,6,1,256]{3,2,1,0:T(2,128)(2,1)S(1)}, bf16[8,6,1,256]{3,2,1,0:T(2,128)(2,1)S(1)}, u32[]{:S(2)}, u32[]{:S(2)}) collective-permute-start(bf16[8,6,1,256]{3,2,1,0:T(2,128)(2,1)S(1)} %get-tuple-element.168), channel_id=1, source_target_pairs={{0,1},{2,3},{4,5},{6,7},{8,9},{10,11},{12,13},{14,15},{16,17},{18,... | collective-permute-start | bytes 73736 | tf_op jit(solution)/shard_map/ppermute | solution.py:15
  92.9 5.2 %collective-permute-start.15 = (bf16[8,6,1,256]{3,2,1,0:T(2,128)(2,1)S(1)}, bf16[8,6,1,256]{3,2,1,0:T(2,128)(2,1)S(1)}, u32[]{:S(2)}, u32[]{:S(2)}) collective-permute-start(bf16[8,6,1,256]{3,2,1,0:T(2,128)(2,1)S(1)} %get-tuple-element.169), channel_id=1, source_target_pairs={{1,0},{3,2},{5,4},{7,6},{9,8},{11,10},{13,12},{15,14},{17,16},{19,... | collective-permute-start | bytes 73736 | tf_op jit(solution)/shard_map/ppermute | solution.py:17
  98.1 3.5 %copy-start.10 = (bf16[8,6,1,256]{3,2,1,0:T(2,128)(2,1)}, bf16[8,6,1,256]{3,2,1,0:T(2,128)(2,1)S(1)}, u32[]{:S(2)}) copy-start(bf16[8,6,1,256]{3,2,1,0:T(2,128)(2,1)S(1)} %collective-permute-done.15) | copy-start | bytes 73732
  104.8 5.9 %copy-start.9 = (bf16[128,256]{1,0:T(8,128)(2,1)S(1)}, bf16[128,256]{1,0:T(8,128)(2,1)}, u32[]{:S(2)}) copy-start(bf16[128,256]{1,0:T(8,128)(2,1)} %reshape.512) | copy-start | bytes 196612
  121.1 6.7 %collective-permute-start.16 = (bf16[8,1,4,512]{3,2,1,0:T(4,128)(2,1)S(1)}, bf16[8,1,4,512]{3,2,1,0:T(4,128)(2,1)S(1)}, u32[]{:S(2)}, u32[]{:S(2)}) collective-permute-start(bf16[8,1,4,512]{3,2,1,0:T(4,128)(2,1)S(1)} %get-tuple-element.154), channel_id=1, source_target_pairs={{0,2},{2,4},{4,6},{1,3},{3,5},{5,7},{8,10},{10,12},{12,14},{9,11},... | collective-permute-start | bytes 98312 | tf_op jit(solution)/shard_map/ppermute | solution.py:15
  125.9 5.2 %collective-permute-start.17 = (bf16[8,1,4,512]{3,2,1,0:T(4,128)(2,1)S(1)}, bf16[8,1,4,512]{3,2,1,0:T(4,128)(2,1)S(1)}, u32[]{:S(2)}, u32[]{:S(2)}) collective-permute-start(bf16[8,1,4,512]{3,2,1,0:T(4,128)(2,1)S(1)} %get-tuple-element.153), channel_id=1, source_target_pairs={{2,0},{4,2},{6,4},{3,1},{5,3},{7,5},{10,8},{12,10},{14,12},{11,9},... | collective-permute-start | bytes 98312 | tf_op jit(solution)/shard_map/ppermute | solution.py:17
  131.5 7.1 %collective-permute-start.18 = (bf16[8,6,1,512]{3,2,1,0:T(2,128)(2,1)S(1)}, bf16[8,6,1,512]{3,2,1,0:T(2,128)(2,1)S(1)}, u32[]{:S(2)}, u32[]{:S(2)}) collective-permute-start(bf16[8,6,1,512]{3,2,1,0:T(2,128)(2,1)S(1)} %get-tuple-element.142), channel_id=1, source_target_pairs={{0,1},{2,3},{4,5},{6,7},{8,9},{10,11},{12,13},{14,15},{16,17},{18,... | collective-permute-start | bytes 147464 | tf_op jit(solution)/shard_map/ppermute | solution.py:15
  132.8 5.8 %collective-permute-start.19 = (bf16[8,6,1,512]{3,2,1,0:T(2,128)(2,1)S(1)}, bf16[8,6,1,512]{3,2,1,0:T(2,128)(2,1)S(1)}, u32[]{:S(2)}, u32[]{:S(2)}) collective-permute-start(bf16[8,6,1,512]{3,2,1,0:T(2,128)(2,1)S(1)} %get-tuple-element.143), channel_id=1, source_target_pairs={{1,0},{3,2},{5,4},{7,6},{9,8},{11,10},{13,12},{15,14},{17,16},{19,... | collective-permute-start | bytes 147464 | tf_op jit(solution)/shard_map/ppermute | solution.py:17
  138.6 0.6 copy-start.4
  139.2 0.6 copy-start.5
  149.7 2.6 %copy-start.8 = (f32[128,128]{1,0:T(8,128)S(1)}, f32[128,128]{1,0:T(8,128)}, u32[]{:S(2)}) copy-start(f32[128,128]{1,0:T(8,128)} %fusion.169) | copy-start | bytes 196612
  152.3 9.9 %copy-start.7 = (f32[128,128]{1,0:T(8,128)S(1)}, f32[128,128]{1,0:T(8,128)}, u32[]{:S(2)}) copy-start(f32[128,128]{1,0:T(8,128)} %fusion.157) | copy-start | bytes 196612
  156.7 9.8 %copy-start.6 = (f32[128,128]{1,0:T(8,128)S(1)}, f32[128,128]{1,0:T(8,128)}, u32[]{:S(2)}) copy-start(f32[128,128]{1,0:T(8,128)} %fusion.151) | copy-start | bytes 196612
  183.7 5.0 %collective-permute-start.20 = (bf16[1,8,8,768]{3,2,1,0:T(8,128)(2,1)S(1)}, bf16[1,8,8,768]{3,2,1,0:T(8,128)(2,1)S(1)}, u32[]{:S(2)}, u32[]{:S(2)}) collective-permute-start(bf16[1,8,8,768]{3,2,1,0:T(8,128)(2,1)S(1)} %get-tuple-element.95), channel_id=1, source_target_pairs={{0,8},{8,16},{16,24},{1,9},{9,17},{17,25},{2,10},{10,18},{18,26},{... | collective-permute-start | bytes 294920 | tf_op jit(solution)/shard_map/ppermute | solution.py:15
  186.1 6.4 %collective-permute-start.21 = (bf16[1,8,8,768]{3,2,1,0:T(8,128)(2,1)S(1)}, bf16[1,8,8,768]{3,2,1,0:T(8,128)(2,1)S(1)}, u32[]{:S(2)}, u32[]{:S(2)}) collective-permute-start(bf16[1,8,8,768]{3,2,1,0:T(8,128)(2,1)S(1)} %get-tuple-element.96), channel_id=1, source_target_pairs={{8,0},{16,8},{24,16},{9,1},{17,9},{25,17},{10,2},{18,10},{26,18},{... | collective-permute-start | bytes 294920 | tf_op jit(solution)/shard_map/ppermute | solution.py:17
  193.8 7.2 %collective-permute-start.22 = (bf16[6,1,8,768]{3,2,1,0:T(8,128)(2,1)S(1)}, bf16[6,1,8,768]{3,2,1,0:T(8,128)(2,1)S(1)}, u32[]{:S(2)}, u32[]{:S(2)}) collective-permute-start(bf16[6,1,8,768]{3,2,1,0:T(8,128)(2,1)S(1)} %get-tuple-element.68), channel_id=1, source_target_pairs={{0,2},{2,4},{4,6},{1,3},{3,5},{5,7},{8,10},{10,12},{12,14},{9,11},... | collective-permute-start | bytes 221192 | tf_op jit(solution)/shard_map/ppermute | solution.py:15
  197.8 5.7 %collective-permute-start.23 = (bf16[6,1,8,768]{3,2,1,0:T(8,128)(2,1)S(1)}, bf16[6,1,8,768]{3,2,1,0:T(8,128)(2,1)S(1)}, u32[]{:S(2)}, u32[]{:S(2)}) collective-permute-start(bf16[6,1,8,768]{3,2,1,0:T(8,128)(2,1)S(1)} %get-tuple-element.69), channel_id=1, source_target_pairs={{2,0},{4,2},{6,4},{3,1},{5,3},{7,5},{10,8},{12,10},{14,12},{11,9},... | collective-permute-start | bytes 221192 | tf_op jit(solution)/shard_map/ppermute | solution.py:17
  203.8 13.8 %collective-permute-start.24 = (bf16[6,10,1,768]{3,2,1,0:T(2,128)(2,1)S(1)}, bf16[6,10,1,768]{3,2,1,0:T(2,128)(2,1)S(1)}, u32[]{:S(2)}, u32[]{:S(2)}) collective-permute-start(bf16[6,10,1,768]{3,2,1,0:T(2,128)(2,1)S(1)} %get-tuple-element.44), channel_id=1, source_target_pairs={{0,1},{2,3},{4,5},{6,7},{8,9},{10,11},{12,13},{14,15},{16,17},{18,... | collective-permute-start | bytes 276488 | tf_op jit(solution)/shard_map/ppermute | solution.py:15
  205.1 12.5 %collective-permute-start.25 = (bf16[6,10,1,768]{3,2,1,0:T(2,128)(2,1)S(1)}, bf16[6,10,1,768]{3,2,1,0:T(2,128)(2,1)S(1)}, u32[]{:S(2)}, u32[]{:S(2)}) collective-permute-start(bf16[6,10,1,768]{3,2,1,0:T(2,128)(2,1)S(1)} %get-tuple-element.43), channel_id=1, source_target_pairs={{1,0},{3,2},{5,4},{7,6},{9,8},{11,10},{13,12},{15,14},{17,16},{19,... | collective-permute-start | bytes 276488 | tf_op jit(solution)/shard_map/ppermute | solution.py:17
  209.4 9.9 %slice-start = ((s8[10616832]{0:T(1024)(128)(4,1)}), s8[4194304]{0:T(1024)(128)(4,1)S(1)}, s32[]{:S(2)}) async-start(s8[10616832]{0:T(1024)(128)(4,1)} %bitcast.633), calls=%async_computation.1 | async-start | bytes 8388608
  212.3 7.0 %slice-start.1 = ((s8[10616832]{0:T(1024)(128)(4,1)}), s8[4194304]{0:T(1024)(128)(4,1)S(1)}, s32[]{:S(2)}) async-start(s8[10616832]{0:T(1024)(128)(4,1)} %bitcast.633), calls=%async_computation.2 | async-start | bytes 8388608
  217.6 1.8 slice-start.2
